TPU v7x, 8 devices: a whole 2x2x1 slice. The times are simulated.
8 devices in a mesh: dp: 2 (over z, y), ep: 4 (over x, core).
Axes of the slice: x: 2, y: 2, z: 1, core: 2. Of those that a mesh axis runs over, the one named last changes fastest.
Arguments:
- x_tokens: bfloat16 [512, 1536], P(('dp', 'ep')), parts along dimension 0
- dy_tokens: bfloat16 [512, 1536], P(('dp', 'ep')), parts along dimension 0
- expert_ids: int32 [512, 8], P(('dp', 'ep')), parts along dimension 0
- gate_vals: float32 [512, 8], P(('dp', 'ep')), parts along dimension 0
- slot_ids: int32 [512, 8], P(('dp', 'ep')), parts along dimension 0
- w_gate: bfloat16 [40, 1536, 512], P('ep')
- w_down: bfloat16 [40, 512, 1536], P('ep')
- w_up: bfloat16 [40, 1536, 512], P('ep')
Outputs:
- output 1: bfloat16 [512, 1536], P(('dp', 'ep')), parts along dimension 0
- output 2: float32 [80, 1536, 512], P(('dp', 'ep')), parts along dimension 0
- output 3: float32 [80, 512, 1536], P(('dp', 'ep')), parts along dimension 0
- output 4: float32 [80, 1536, 512], P(('dp', 'ep')), parts along dimension 0
There are 2 independent parts. A program takes and returns all parts, laid end to end along the dimension named above; an argument that names none is the same for every part.
All inputs are finite; a program needn't handle non-finite values.
Results may differ from a plain program's by a relative error of at most 0.010384.
Values are sent between devices in bfloat16 or wider.
A program may use at most 1 GiB of HBM per device.

v0:
```python
import jax
import jax.numpy as jnp
from jax import lax
from jax.sharding import PartitionSpec as P


def slot_capacity(tok_dev, top_k, n_exp):
    return ((3 * tok_dev * top_k) // (2 * n_exp) + 7) // 8 * 8


def source_dispatch(x_src, dy_src, ids_src, gate_src, slot_src, cap_rows, n_exp):
    tok_dev, top_k = ids_src.shape
    n_copy = tok_dev * top_k
    d_model = x_src.shape[1]
    flat_slot = jnp.where(slot_src >= 0, ids_src * cap_rows + slot_src, n_exp * cap_rows)
    slot_copy = jnp.full((n_exp * cap_rows,), n_copy, jnp.int32).at[flat_slot.reshape(n_copy)].set(jnp.arange(n_copy, dtype=jnp.int32), mode='drop')
    slot_tok = slot_copy // top_k
    x_send = jnp.take(x_src, slot_tok, axis=0, mode='fill', fill_value=0)
    dy_send = jnp.take(dy_src, slot_tok, axis=0, mode='fill', fill_value=0)
    gate_slot = jnp.take(gate_src.reshape(n_copy), slot_copy, mode='fill', fill_value=0)
    dz_send = (gate_slot[:, None] * dy_send).astype(jnp.bfloat16)
    return x_send.reshape(n_exp, cap_rows, d_model), dz_send.reshape(n_exp, cap_rows, d_model), flat_slot


def source_combine(dx_send, flat_slot):
    n_exp, cap_rows, d_model = dx_send.shape
    rows = jnp.take(dx_send.reshape(n_exp * cap_rows, d_model), flat_slot, axis=0, mode='fill', fill_value=0)
    return jnp.sum(rows, axis=1, dtype=jnp.float32).astype(jnp.bfloat16)


def expert_backward(x_rows, dz_rows, w_gate, w_down, w_up):
    a_pre = jnp.einsum('erd,edf->erf', x_rows, w_gate, preferred_element_type=jnp.float32).astype(jnp.bfloat16).astype(jnp.float32)
    b_pre = jnp.einsum('erd,edf->erf', x_rows, w_up, preferred_element_type=jnp.float32).astype(jnp.bfloat16).astype(jnp.float32)
    sigma_a = jax.nn.sigmoid(a_pre)
    silu_a = a_pre * sigma_a
    hidden = (silu_a * b_pre).astype(jnp.bfloat16)
    d_hidden = jnp.einsum('erd,efd->erf', dz_rows, w_down, preferred_element_type=jnp.float32)
    d_gate = (d_hidden * b_pre * sigma_a * (1.0 + a_pre * (1.0 - sigma_a))).astype(jnp.bfloat16)
    d_up = (d_hidden * silu_a).astype(jnp.bfloat16)
    g_down = jnp.einsum('erf,erd->efd', hidden, dz_rows, preferred_element_type=jnp.float32)
    g_gate = jnp.einsum('erd,erf->edf', x_rows, d_gate, preferred_element_type=jnp.float32)
    g_up = jnp.einsum('erd,erf->edf', x_rows, d_up, preferred_element_type=jnp.float32)
    dx_rows = (jnp.einsum('erf,edf->erd', d_gate, w_gate, preferred_element_type=jnp.float32) + jnp.einsum('erf,edf->erd', d_up, w_up, preferred_element_type=jnp.float32)).astype(jnp.bfloat16)
    return dx_rows, g_gate, g_down, g_up


def solution(mesh):
    n_dev = mesh.shape['ep']

    def local_step(x_loc, dy_loc, ids_loc, gate_loc, slot_loc, w_gate, w_down, w_up):
        tok_dev, top_k = ids_loc.shape
        n_local = w_gate.shape[0]
        n_exp = n_local * n_dev
        d_model = x_loc.shape[1]
        cap_rows = slot_capacity(tok_dev, top_k, n_exp)
        x_send, dz_send, flat_slot = source_dispatch(x_loc, dy_loc, ids_loc, gate_loc, slot_loc, cap_rows, n_exp)
        x_recv = lax.all_to_all(x_send.reshape(n_exp, 1, cap_rows, d_model), 'ep', 0, 1, tiled=True)
        dz_recv = lax.all_to_all(dz_send.reshape(n_exp, 1, cap_rows, d_model), 'ep', 0, 1, tiled=True)
        dx_rows, g_gate, g_down, g_up = expert_backward(x_recv.reshape(n_local, n_dev * cap_rows, d_model), dz_recv.reshape(n_local, n_dev * cap_rows, d_model), w_gate, w_down, w_up)
        dx_back = lax.all_to_all(dx_rows.reshape(n_local, n_dev, cap_rows, d_model), 'ep', 1, 0, tiled=True)
        dx_loc = source_combine(dx_back.reshape(n_exp, cap_rows, d_model), flat_slot)
        return dx_loc, g_gate, g_down, g_up

    tok_spec = P(('dp', 'ep'), None)
    w_spec = P('ep', None, None)
    grad_spec = P(('dp', 'ep'), None, None)
    return jax.shard_map(local_step, mesh=mesh, in_specs=(tok_spec, tok_spec, tok_spec, tok_spec, tok_spec, w_spec, w_spec, w_spec), out_specs=(tok_spec, grad_spec, grad_spec, grad_spec), check_vma=False)
```

profile of v0, /device:TPU:0, one launch (start us, length us, event | category | flops | bytes accessed | tf_op | source)
XLA Modules:
  0.0 195.6 jit_solution(4694099254532792933)
XLA Ops:
  0.6 0.8 compare_and_fusion.1
  1.5 0.1 reshape.71
  1.6 2.4 %scatter_custom_fusion = s32[960]{0:T(1024)S(1)} fusion(s32[512]{0:T(512)S(1)} %bitcast.49, s32[512]{0:T(512)S(1)} %iota.3, s32[]{:T(128)} %constant.58.clone.1), kind=kCustom, calls=%fused_computation.45 | custom fusion | bytes 3844 | tf_op jit(solution)/shard_map/scatter | solution.py:16
  4.1 5.5 %gather_fusion.3 = bf16[960,1536]{1,0:T(8,128)(2,1)} fusion(bf16[64,1536]{1,0:T(8,128)(2,1)S(1)} %copy-done, s32[1024]{0:T(1024)S(1)} %pad_clamp_fusion.1), kind=kCustom, calls=%fused_computation.1.clone | custom fusion | bytes 5902080 | tf_op jit(solution)/shard_map/jit(_take)/gather | solution.py:18
  9.6 3.7 %broadcast_select_fusion = bf16[960,1536]{1,0:T(8,128)(2,1)} fusion(bf16[960,1536]{1,0:T(8,128)(2,1)} %gather_fusion.3, pred[960]{0:T(1024)(128)(4,1)S(1)} %get-tuple-element.7), kind=kLoop, calls=%fused_computation.10 | loop fusion | flops 1474560 | bytes 5899200 | tf_op jit(solution)/shard_map/jit(_take)/select_n | solution.py:18
  13.3 4.7 %all-to-all-start.1 = ((bf16[40,1,24,1536]{3,2,1,0:T(8,128)(2,1)}), bf16[40,1,24,1536]{3,2,1,0:T(8,128)(2,1)}, u32[]{:S(2)}, u32[]{:S(2)}) async-start(bf16[40,1,24,1536]{3,2,1,0:T(8,128)(2,1)} %bitcast.48), calls=%async_computation.1 | async-start | bytes 5898240 | tf_op jit(solution)/shard_map/all_to_all | solution.py:57
  18.1 0.1 copy.23
  18.1 0.1 reshape.72
  18.2 5.5 %gather_fusion.2 = bf16[960,1536]{1,0:T(8,128)(2,1)} fusion(bf16[64,1536]{1,0:T(8,128)(2,1)S(1)} %copy-done.2, s32[1024]{0:T(1024)S(1)} %pad_clamp_fusion.1), kind=kCustom, calls=%fused_computation.clone | custom fusion | bytes 5902080 | tf_op jit(solution)/shard_map/jit(_take)/gather | solution.py:19
  23.8 6.5 %gather_fusion = f32[960]{0:T(1024)S(1)} fusion(f32[512]{0:T(512)S(1)} %reshape.72, s32[1024]{0:T(1024)S(1)} %pad_clamp_fusion.2), kind=kCustom, calls=%fused_computation.2 | custom fusion | bytes 11520 | tf_op jit(solution)/shard_map/jit(_take)/gather | solution.py:20
  30.3 3.5 %multiply_convert_fusion = bf16[960,1536]{1,0:T(8,128)(2,1)} fusion(bf16[960,1536]{1,0:T(8,128)(2,1)} %gather_fusion.2, f32[960]{0:T(1024)S(1)} %and_select_fusion, pred[960]{0:T(1024)(128)(4,1)S(1)} %get-tuple-element.7), kind=kLoop, calls=%fused_computation.6 | loop fusion | flops 5898240 | bytes 5903040 | tf_op jit(solution)/shard_map/convert_element_type | solution.py:21
  33.7 19.9 %all-to-all-done.1 = bf16[40,1,24,1536]{3,2,1,0:T(8,128)(2,1)} async-done(((bf16[40,1,24,1536]{3,2,1,0:T(8,128)(2,1)}), bf16[40,1,24,1536]{3,2,1,0:T(8,128)(2,1)}, u32[]{:S(2)}, u32[]{:S(2)}) %all-to-all-start.1) | async-done | bytes 2949152 | tf_op jit(solution)/shard_map/all_to_all | solution.py:57
  53.7 4.8 %all-to-all-start = ((bf16[40,1,24,1536]{3,2,1,0:T(8,128)(2,1)}), bf16[40,1,24,1536]{3,2,1,0:T(8,128)(2,1)}, u32[]{:S(2)}, u32[]{:S(2)}) async-start(bf16[40,1,24,1536]{3,2,1,0:T(8,128)(2,1)} %bitcast.2), calls=%async_computation | async-start | bytes 5898240 | tf_op jit(solution)/shard_map/all_to_all | solution.py:58
  58.5 0.1 copy.21
  58.7 0.1 reshape.102
  58.8 2.3 %copy.27 = bf16[10,4,1,24,1536]{4,3,1,0,2:T(8,128)(2,1)S(1)} copy(bf16[10,4,1,24,1536]{4,3,0,1,2:T(8,128)(2,1)} %bitcast.9) | data formatting | bytes 5898240 | tf_op jit(solution)/shard_map/all_to_all | solution.py:57
  61.1 9.2 %convolution_convert_fusion = bf16[10,96,512]{2,1,0:T(8,128)(2,1)} fusion(bf16[10,96,1536]{2,1,0:T(8,128)(2,1)S(1)} %bitcast.39, bf16[10,1536,512]{2,1,0:T(8,128)(2,1)} %param.15), kind=kOutput, calls=%fused_computation.24 | convolution fusion | flops 1510440960 | bytes 19660800 | tf_op jit(solution)/shard_map/erd,edf->erf/dot_general | solution.py:32
  70.4 3.5 %convolution_convert_fusion.1 = bf16[10,96,512]{2,1,0:T(8,128)(2,1)} fusion(bf16[10,96,1536]{2,1,0:T(8,128)(2,1)S(1)} %bitcast.40, bf16[10,1536,512]{2,1,0:T(8,128)(2,1)S(1)} %bitcast.44), kind=kOutput, calls=%fused_computation.25 | convolution fusion | flops 1510440960 | bytes 19660800 | tf_op jit(solution)/shard_map/erd,edf->erf/dot_general | solution.py:33
  73.9 18.9 %all-to-all-done = bf16[40,1,24,1536]{3,2,1,0:T(8,128)(2,1)} async-done(((bf16[40,1,24,1536]{3,2,1,0:T(8,128)(2,1)}), bf16[40,1,24,1536]{3,2,1,0:T(8,128)(2,1)}, u32[]{:S(2)}, u32[]{:S(2)}) %all-to-all-start) | async-done | bytes 2949152 | tf_op jit(solution)/shard_map/all_to_all | solution.py:58
  92.9 2.2 %copy.25 = bf16[10,4,1,24,1536]{4,3,1,0,2:T(8,128)(2,1)S(1)} copy(bf16[10,4,1,24,1536]{4,3,0,1,2:T(8,128)(2,1)} %bitcast.4) | data formatting | bytes 5898240 | tf_op jit(solution)/shard_map/all_to_all | solution.py:58
  95.1 1.6 copy-done.6
  96.7 13.3 %fusion.9 = f32[10,512,1536]{2,1,0:T(8,128)} fusion(bf16[10,96,1536]{2,1,0:T(8,128)(2,1)S(1)} %bitcast.46, bf16[10,96,512]{2,1,0:T(8,128)(2,1)S(1)} %copy-done.7, bf16[10,96,512]{2,1,0:T(8,128)(2,1)S(1)} %copy-done.3), kind=kOutput, calls=%fused_computation.26 | convolution fusion | flops 1513881600 | bytes 36372480 | tf_op jit(solution)/shard_map/erf,erd->efd/dot_general | solution.py:40
  110.0 13.4 %fusion.2 = (bf16[10,96,512]{2,1,0:T(8,128)(2,1)}, f32[10,96,512]{2,1,0:T(8,128)}) fusion(bf16[10,96,512]{2,1,0:T(8,128)(2,1)} %convolution_convert_fusion.1, bf16[10,96,512]{2,1,0:T(8,128)(2,1)} %convolution_convert_fusion, bf16[10,96,1536]{2,1,0:T(8,128)(2,1)} %bitcast.47, bf16[10,512,1536]{2,1,0:T(8,128)(2,1)} %param.16), kind=kOutput, calls=%fused_computation.15 | convolution fusion | flops 1515847680 | bytes 23592960 | tf_op jit(solution)/shard_map/erd,efd->erf/dot_general | solution.py:37
  123.4 13.2 %fusion.17 = f32[10,96,1536]{2,1,0:T(8,128)} fusion(bf16[10,96,512]{2,1,0:T(8,128)(2,1)} %get-tuple-element.9, bf16[10,1536,512]{2,1,0:T(8,128)(2,1)} %param.15), kind=kOutput, calls=%fused_computation.49 | convolution fusion | flops 1509949440 | bytes 22609920 | tf_op jit(solution)/shard_map/erf,edf->erd/dot_general | solution.py:43
  136.6 10.6 %add_convert_fusion = bf16[10,96,1536]{2,1,0:T(8,128)(2,1)S(1)} fusion(f32[10,96,1536]{2,1,0:T(8,128)} %fusion.17, bf16[10,1536,512]{2,1,0:T(8,128)(2,1)} %param.17, f32[10,96,512]{2,1,0:T(8,128)} %get-tuple-element.10, bf16[10,96,512]{2,1,0:T(8,128)(2,1)} %convolution_convert_fusion), kind=kOutput, calls=%fused_computation.5 | convolution fusion | flops 1516339200 | bytes 27525120 | tf_op jit(solution)/shard_map/erf,edf->erd/dot_general | solution.py:43
  147.2 1.9 copy.28
  149.1 4.6 %all-to-all-start.2 = ((bf16[10,4,24,1536]{3,2,0,1:T(8,128)(2,1)}), bf16[10,4,24,1536]{3,2,0,1:T(8,128)(2,1)}, u32[]{:S(2)}, u32[]{:S(2)}) async-start(bf16[10,4,24,1536]{3,2,0,1:T(8,128)(2,1)} %copy.28), calls=%async_computation.2 | async-start | bytes 5898240 | tf_op jit(solution)/shard_map/all_to_all | solution.py:60
  153.7 14.6 %fusion.18 = f32[10,1536,512]{2,1,0:T(8,128)} fusion(bf16[10,96,1536]{2,1,0:T(8,128)(2,1)S(1)} %bitcast.41, bf16[10,96,512]{2,1,0:T(8,128)(2,1)} %get-tuple-element.9), kind=kOutput, calls=%fused_computation.50 | convolution fusion | flops 1509949440 | bytes 35389440 | tf_op jit(solution)/shard_map/erd,erf->edf/dot_general | solution.py:41
  168.3 13.2 %fusion.16 = f32[10,1536,512]{2,1,0:T(8,128)} fusion(bf16[10,96,1536]{2,1,0:T(8,128)(2,1)S(1)} %bitcast.42, f32[10,96,512]{2,1,0:T(8,128)S(1)} %copy-done.5, bf16[10,96,512]{2,1,0:T(8,128)(2,1)S(1)} %copy-done.4), kind=kOutput, calls=%fused_computation.48 | convolution fusion | flops 1513390080 | bytes 37355520 | tf_op jit(solution)/shard_map/erd,erf->edf/dot_general | solution.py:42
  181.6 6.7 %all-to-all-done.2 = bf16[10,4,24,1536]{3,2,0,1:T(8,128)(2,1)} async-done(((bf16[10,4,24,1536]{3,2,0,1:T(8,128)(2,1)}), bf16[10,4,24,1536]{3,2,0,1:T(8,128)(2,1)}, u32[]{:S(2)}, u32[]{:S(2)}) %all-to-all-start.2) | async-done | bytes 2949152 | tf_op jit(solution)/shard_map/all_to_all | solution.py:60
  188.2 5.9 %gather_fusion.1 = bf16[512,1536]{1,0:T(8,128)(2,1)S(1)} fusion(bf16[960,1536]{1,0:T(8,128)(2,1)} %bitcast.14, s32[1024]{0:T(1024)S(1)} %pad_clamp_fusion), kind=kCustom, calls=%fused_computation.3 | custom fusion | bytes 3147776 | tf_op jit(solution)/shard_map/jit(_take)/gather | solution.py:27
  194.1 1.5 fusion.8
  (37 shorter events, 0.3 us)
Async XLA Ops:
  0.6 3.5 %copy-start = (bf16[64,1536]{1,0:T(8,128)(2,1)S(1)}, bf16[64,1536]{1,0:T(8,128)(2,1)}, u32[]{:S(2)}) copy-start(bf16[64,1536]{1,0:T(8,128)(2,1)} %param.10) | copy-start | bytes 589828
  13.3 4.8 %copy-start.8 = (f32[64,8]{0,1:T(8,128)S(1)}, f32[64,8]{0,1:T(8,128)}, u32[]{:S(2)}) copy-start(f32[64,8]{0,1:T(8,128)} %param.13) | copy-start | bytes 6148
  13.3 4.9 %copy-start.2 = (bf16[64,1536]{1,0:T(8,128)(2,1)S(1)}, bf16[64,1536]{1,0:T(8,128)(2,1)}, u32[]{:S(2)}) copy-start(bf16[64,1536]{1,0:T(8,128)(2,1)} %param.11) | copy-start | bytes 589828
  13.3 40.4 %all-to-all-start.1 = ((bf16[40,1,24,1536]{3,2,1,0:T(8,128)(2,1)}), bf16[40,1,24,1536]{3,2,1,0:T(8,128)(2,1)}, u32[]{:S(2)}, u32[]{:S(2)}) async-start(bf16[40,1,24,1536]{3,2,1,0:T(8,128)(2,1)} %bitcast.48), calls=%async_computation.1 | async-start | bytes 5898240 | tf_op jit(solution)/shard_map/all_to_all | solution.py:57
  53.7 39.2 %all-to-all-start = ((bf16[40,1,24,1536]{3,2,1,0:T(8,128)(2,1)}), bf16[40,1,24,1536]{3,2,1,0:T(8,128)(2,1)}, u32[]{:S(2)}, u32[]{:S(2)}) async-start(bf16[40,1,24,1536]{3,2,1,0:T(8,128)(2,1)} %bitcast.2), calls=%async_computation | async-start | bytes 5898240 | tf_op jit(solution)/shard_map/all_to_all | solution.py:58
  58.8 11.6 %slice-start = ((s8[15728640]{0:T(1024)(128)(4,1)}), s8[4194304]{0:T(1024)(128)(4,1)S(1)}, s32[]{:S(2)}) async-start(s8[15728640]{0:T(1024)(128)(4,1)} %bitcast.43), calls=%async_computation.3 | async-start | bytes 8388608
  61.1 9.3 %slice-start.1 = ((s8[15728640]{0:T(1024)(128)(4,1)}), s8[4194304]{0:T(1024)(128)(4,1)S(1)}, s32[]{:S(2)}) async-start(s8[15728640]{0:T(1024)(128)(4,1)} %bitcast.43), calls=%async_computation.4 | async-start | bytes 8388608
  61.1 9.3 %slice-start.2 = ((s8[15728640]{0:T(1024)(128)(4,1)}), s8[4194304]{0:T(1024)(128)(4,1)S(1)}, s32[]{:S(2)}) async-start(s8[15728640]{0:T(1024)(128)(4,1)} %bitcast.43), calls=%async_computation.5 | async-start | bytes 8388608
  61.1 9.3 %slice-start.3 = ((s8[15728640]{0:T(1024)(128)(4,1)}), s8[3145728]{0:T(1024)(128)(4,1)S(1)}, s32[]{:S(2)}) async-start(s8[15728640]{0:T(1024)(128)(4,1)} %bitcast.43), calls=%async_computation.6 | async-start | bytes 6291456
  92.9 3.9 %copy-start.3 = (bf16[10,96,512]{2,1,0:T(8,128)(2,1)S(1)}, bf16[10,96,512]{2,1,0:T(8,128)(2,1)}, u32[]{:S(2)}) copy-start(bf16[10,96,512]{2,1,0:T(8,128)(2,1)} %convolution_convert_fusion) | copy-start | bytes 2949124
  92.9 3.9 %copy-start.7 = (bf16[10,96,512]{2,1,0:T(8,128)(2,1)S(1)}, bf16[10,96,512]{2,1,0:T(8,128)(2,1)}, u32[]{:S(2)}) copy-start(bf16[10,96,512]{2,1,0:T(8,128)(2,1)} %convolution_convert_fusion.1) | copy-start | bytes 2949124
  95.1 1.6 copy-start.6
  149.1 39.2 %all-to-all-start.2 = ((bf16[10,4,24,1536]{3,2,0,1:T(8,128)(2,1)}), bf16[10,4,24,1536]{3,2,0,1:T(8,128)(2,1)}, u32[]{:S(2)}, u32[]{:S(2)}) async-start(bf16[10,4,24,1536]{3,2,0,1:T(8,128)(2,1)} %copy.28), calls=%async_computation.2 | async-start | bytes 5898240 | tf_op jit(solution)/shard_map/all_to_all | solution.py:60
  153.7 14.6 %copy-start.4 = (bf16[10,96,512]{2,1,0:T(8,128)(2,1)S(1)}, bf16[10,96,512]{2,1,0:T(8,128)(2,1)}, u32[]{:S(2)}) copy-start(bf16[10,96,512]{2,1,0:T(8,128)(2,1)} %convolution_convert_fusion) | copy-start | bytes 2949124
  153.7 14.6 %copy-start.5 = (f32[10,96,512]{2,1,0:T(8,128)S(1)}, f32[10,96,512]{2,1,0:T(8,128)}, u32[]{:S(2)}) copy-start(f32[10,96,512]{2,1,0:T(8,128)} %get-tuple-element.10) | copy-start | bytes 5898244
  188.2 7.3 %copy-start.1 = (bf16[64,1536]{1,0:T(8,128)(2,1)S(1)}, bf16[64,1536]{1,0:T(8,128)(2,1)}, u32[]{:S(2)}) copy-start(bf16[64,1536]{1,0:T(8,128)(2,1)} %param.10) | copy-start | bytes 589828
where the time goes:
time: 196 us
  matrix products  91.1 us (46%)
  waiting for transfers between devices  45.5 us (23%)
  local copies, waits for them, and re-layouts  34.5 us (18%)
  starting transfers between devices  14.2 us (7%)
  other arithmetic  9.45 us (5%)
    all_to_all x1, waiting for transfers between devices, local_step(): lax.all_to_all(x_send.reshape(n_exp, 1, cap_rows, d_model), 'ep', 0, 1, t...  19.9 us
    all_to_all x1, waiting for transfers between devices, local_step(): lax.all_to_all(dz_send.reshape(n_exp, 1, cap_rows, d_model), 'ep', 0, 1,...  18.9 us
    dot_general x1, matrix products, expert_backward(): jnp.einsum('erd,erf->edf', x_rows, d_gate, preferred_element_type=jnp.flo...  14.6 us
    dot_general x1, matrix products, expert_backward(): jnp.einsum('erd,efd->erf', dz_rows, w_down, preferred_element_type=jnp.fl...  13.4 us
    dot_general x1, matrix products, expert_backward(): jnp.einsum('erf,erd->efd', hidden, dz_rows, preferred_element_type=jnp.fl...  13.3 us
    dot_general x1, matrix products, expert_backward(): jnp.einsum('erd,erf->edf', x_rows, d_up, preferred_element_type=jnp.float32)  13.2 us
    dot_general x1, matrix products, expert_backward(): jnp.einsum('erf,edf->erd', d_gate, w_gate, preferred_element_type=jnp.flo...  13.2 us
    dot_general x1, matrix products, expert_backward(): jnp.einsum('erf,edf->erd', d_up, w_up, preferred_element_type=jnp.float32)  10.6 us
  transfers between devices with their start and end apart: 3, of which 3 were waited for; matrix products, arithmetic and copies ran while one was open for 30% of the time, Pallas kernels for 0%

commit v1 on v0

v1 whole, which is shorter than its diff:
```python
import functools

import jax
import jax.numpy as jnp
from jax import lax
from jax.experimental import pallas as pl
from jax.experimental.pallas import tpu as pltpu
from jax.sharding import PartitionSpec as P

F32, BF16 = jnp.float32, jnp.bfloat16
TN = (((0,), (0,)), ((), ()))
NT = (((1,), (1,)), ((), ()))


def slot_capacity(tok_dev, top_k, n_exp):
    return ((3 * tok_dev * top_k) // (2 * n_exp) + 7) // 8 * 8


def dot(a, b, dims=None):
    if dims is None:
        return jnp.dot(a, b, preferred_element_type=F32)
    return lax.dot_general(a, b, dims, preferred_element_type=F32)


def build_rows(cap, tok_dev, n_dev, n_local, key_ref, gate_ref, x_ref, dy_ref, hot, x_all, dz_all):
    rows = n_dev * cap
    n_tok = n_dev * tok_dev
    first = lax.axis_index('ep') * n_local
    keys = key_ref[...]
    gates = gate_ref[...]
    source = lax.broadcasted_iota(jnp.int32, (1, n_tok), 1) // tok_dev * cap
    row_ids = lax.broadcasted_iota(jnp.int32, (rows, n_tok), 0)
    for e in range(n_local):
        d = keys - (first + e) * cap
        hit = (d >= 0) & (d < cap)
        slot = jnp.sum(jnp.where(hit, d + 1, 0), axis=0, keepdims=True) - 1
        gmap = jnp.sum(jnp.where(hit, gates, 0.0), axis=0, keepdims=True)
        slot = jnp.where(slot >= 0, slot + source, -1)
        mask = row_ids == slot
        gcol = jnp.sum(jnp.where(mask, gmap, 0.0), axis=1, keepdims=True)
        sel = jnp.where(mask, 1.0, 0.0).astype(BF16)
        hot[pl.ds(e * rows, rows), :] = sel
        x_all[e] = dot(sel, x_ref[...]).astype(BF16)
        dz_all[e] = (gcol * dot(sel, dy_ref[...])).astype(BF16)


def expert_kernel(cfg, key_ref, gate_ref, x_ref, dy_ref, w1_ref, w2_ref, w3_ref,
                  part_ref, dw1_ref, dw2_ref, dw3_ref, hot, x_all, dz_all, dx_all):
    cap, tok_dev, n_dev, n_local = cfg
    rows = n_dev * cap
    i = pl.program_id(0)

    @pl.when(i == 0)
    def _():
        build_rows(cap, tok_dev, n_dev, n_local, key_ref, gate_ref, x_ref, dy_ref, hot, x_all, dz_all)

    x = x_all[i]
    dz = dz_all[i]
    a = dot(x, w1_ref[0]).astype(BF16).astype(F32)
    b = dot(x, w3_ref[0]).astype(BF16).astype(F32)
    sg = jax.nn.sigmoid(a)
    silu = a * sg
    h = (silu * b).astype(BF16)
    dh = dot(dz, w2_ref[0], NT)
    da = (dh * b * sg * (1.0 + a * (1.0 - sg))).astype(BF16)
    db = (dh * silu).astype(BF16)
    dx = (dot(da, w1_ref[0], NT) + dot(db, w3_ref[0], NT)).astype(BF16)
    dx_all[pl.ds(pl.multiple_of(i * rows, 16), rows), :] = dx
    d_model = x.shape[1]
    ff = h.shape[1]
    for c in range(d_model // 256):
        xt = x_all[i, :, pl.ds(c * 256, 256)]
        dw1_ref[0, pl.ds(c * 256, 256), :] = dot(xt, da, TN)
        dw3_ref[0, pl.ds(c * 256, 256), :] = dot(xt, db, TN)
    for c in range(ff // 256):
        dw2_ref[0, pl.ds(c * 256, 256), :] = dot(h[:, c * 256:(c + 1) * 256], dz, TN)

    @pl.when(i == n_local - 1)
    def _():
        part_ref[...] = dot(hot[...], dx_all[...], TN)


def solution(mesh):
    n_dev = mesh.shape['ep']

    def local_step(x_loc, dy_loc, ids_loc, gate_loc, slot_loc, w_gate, w_down, w_up):
        tok_dev, top_k = ids_loc.shape
        n_local, d_model, ff = w_gate.shape
        n_exp = n_local * n_dev
        n_tok = tok_dev * n_dev
        cap = slot_capacity(tok_dev, top_k, n_exp)
        rows = n_dev * cap
        keys = jnp.where(slot_loc >= 0, ids_loc * cap + slot_loc, -1).T
        keys = lax.all_gather(keys, 'ep', axis=1, tiled=True)
        gates = lax.all_gather(gate_loc.T, 'ep', axis=1, tiled=True)
        x_tok = lax.all_gather(x_loc, 'ep', axis=0, tiled=True)
        dy_tok = lax.all_gather(dy_loc, 'ep', axis=0, tiled=True)
        whole = lambda shape: pl.BlockSpec(shape, lambda i: (0,) * len(shape))
        per = lambda shape: pl.BlockSpec((1,) + shape, lambda i: (i, 0, 0))
        part, g1, g2, g3 = pl.pallas_call(
            functools.partial(expert_kernel, (cap, tok_dev, n_dev, n_local)),
            grid=(n_local,),
            out_shape=[
                jax.ShapeDtypeStruct((n_tok, d_model), F32),
                jax.ShapeDtypeStruct((n_local, d_model, ff), F32),
                jax.ShapeDtypeStruct((n_local, ff, d_model), F32),
                jax.ShapeDtypeStruct((n_local, d_model, ff), F32),
            ],
            in_specs=[whole((top_k, n_tok)), whole((top_k, n_tok)), whole((n_tok, d_model)), whole((n_tok, d_model)),
                      per((d_model, ff)), per((ff, d_model)), per((d_model, ff))],
            out_specs=[whole((n_tok, d_model)), per((d_model, ff)), per((ff, d_model)), per((d_model, ff))],
            scratch_shapes=[
                pltpu.VMEM((n_local * rows, n_tok), BF16),
                pltpu.VMEM((n_local, rows, d_model), BF16),
                pltpu.VMEM((n_local, rows, d_model), BF16),
                pltpu.VMEM((n_local * rows, d_model), BF16),
            ],
            compiler_params=pltpu.CompilerParams(dimension_semantics=('arbitrary',), vmem_limit_bytes=62 * 1024 * 1024),
            cost_estimate=pl.CostEstimate(flops=16 * n_local * rows * d_model * ff, bytes_accessed=18 * n_local * d_model * ff, transcendentals=0),
            name='experts',
        )(keys, gates, x_tok, dy_tok, w_gate, w_down, w_up)
        dx = lax.psum_scatter(part, 'ep', scatter_dimension=0, tiled=True).astype(BF16)
        return dx, g1, g2, g3

    tok_spec = P(('dp', 'ep'), None)
    w_spec = P('ep', None, None)
    grad_spec = P(('dp', 'ep'), None, None)
    return jax.shard_map(local_step, mesh=mesh, in_specs=(tok_spec, tok_spec, tok_spec, tok_spec, tok_spec, w_spec, w_spec, w_spec), out_specs=(tok_spec, grad_spec, grad_spec, grad_spec), check_vma=False)
```

time: 196 us -> 139 us (0.71)
  matrix products: 91.1 us -> 0 us
  Pallas kernels: 0 us -> 56.6 us
  blocking collectives: 0 us -> 39.9 us
  local copies, waits for them, and re-layouts: 34.5 us -> 1.37 us
  waiting for transfers between devices: 45.5 us -> 24 us
  starting transfers between devices: 14.2 us -> 0.04 us
  between operations: 0.86 us -> 14 us
  other arithmetic: 9.45 us -> 2.4 us
    dot_general x8 -> x0, matrix products: 91.1 us -> none  [the longest x1 14.6 us: expert_backward(): jnp.einsum('erd,erf->edf', x_rows, d_gate, preferred_element_type=jnp.flo...]
    pallas_call x0 -> x1, Pallas kernels: none -> 56.6 us  [local_step(): pl.pallas_call(functools.partial(expert_kernel, (cap, tok_dev, n_dev, n_l...]
    all_to_all x3 -> x0, waiting for transfers between devices: 45.5 us -> none  [the longest x1 19.9 us: local_step(): lax.all_to_all(x_send.reshape(n_exp, 1, cap_rows, d_model), 'ep', 0, 1, t...]
    all_gather x0 -> x4, blocking collectives: none -> 39.9 us  [the longest x1 11.5 us: local_step(): dy_tok = lax.all_gather(dy_loc, 'ep', axis=0, tiled=True)]
    reduce_scatter x0 -> x1, waiting for transfers between devices: none -> 24 us  [local_step(): lax.psum_scatter(part, 'ep', scatter_dimension=0, tiled=True).astype(BF16)]
    gather x4 -> x0, local copies, waits for them, and re-layouts: 23.4 us -> none  [the longest x1 6.52 us: source_dispatch(): jnp.take(gate_src.reshape(n_copy), slot_copy, mode='fill', fill_value=0)]
    all_to_all x3 -> x0, starting transfers between devices: 14.2 us -> none  [the longest x1 4.8 us: local_step(): lax.all_to_all(dz_send.reshape(n_exp, 1, cap_rows, d_model), 'ep', 0, 1,...]
    all_to_all x2 -> x0, local copies, waits for them, and re-layouts: 4.52 us -> none  [the longest x1 2.28 us: local_step(): lax.all_to_all(x_send.reshape(n_exp, 1, cap_rows, d_model), 'ep', 0, 1, t...]
  transfers between devices with their start and end apart: 3 -> 1, of which waited for: 3 -> 1; matrix products, arithmetic and copies ran while one was open for 30% -> 0% of each run, Pallas kernels for 0% -> 0%
where the time goes in v1:
time: 139 us; the launch traced here: 138 us
  Pallas kernels  56.6 us (41%)
  blocking collectives  39.9 us (29%)
  waiting for transfers between devices  24 us (17%)
  between operations  14 us (10%)
  other arithmetic  2.4 us (2%)
    pallas_call x1, Pallas kernels, local_step(): pl.pallas_call(functools.partial(expert_kernel, (cap, tok_dev, n_dev, n_l...  56.6 us
    reduce_scatter x1, waiting for transfers between devices, local_step(): lax.psum_scatter(part, 'ep', scatter_dimension=0, tiled=True).astype(BF16)  24 us
    all_gather x1, blocking collectives, local_step(): dy_tok = lax.all_gather(dy_loc, 'ep', axis=0, tiled=True)  11.5 us
    all_gather x1, blocking collectives, local_step(): x_tok = lax.all_gather(x_loc, 'ep', axis=0, tiled=True)  11.2 us
    all_gather x1, blocking collectives, local_step(): keys = lax.all_gather(keys, 'ep', axis=1, tiled=True)  9.97 us
    all_gather x1, blocking collectives, local_step(): gates = lax.all_gather(gate_loc.T, 'ep', axis=1, tiled=True)  7.3 us
  transfers between devices with their start and end apart: 1, of which 1 were waited for; matrix products, arithmetic and copies ran while one was open for 0% of the time, Pallas kernels for 0%

profile of v1, /device:TPU:0, one launch (start us, length us, event | category | flops | bytes accessed | tf_op | source)
XLA Modules:
  0.0 138.4 jit_solution(17363207934388907009)
XLA Ops:
  7.2 0.0 reduce-scatter.2.cloned.1.call-start
  7.2 0.7 select_bitcast_fusion
  7.9 10.0 %all-gather = s32[4,64,8]{1,2,0:T(8,128)S(1)} all-gather(s32[1,64,8]{1,2,0:T(8,128)S(1)} %select_bitcast_fusion), channel_id=1, replica_groups=mesh['dp'=2,'ep'=4] {'ep'}, dimensions={0}, use_global_device_ids=true | all-gather | bytes 10240 | tf_op jit(solution)/shard_map/all_gather | solution.py:94
  17.9 0.7 reshape.9
  18.6 7.3 %all-gather.1 = f32[4,64,8]{1,2,0:T(8,128)S(1)} all-gather(f32[1,64,8]{1,2,0:T(8,128)} %bitcast.11), channel_id=1, replica_groups=mesh['dp'=2,'ep'=4] {'ep'}, dimensions={0}, use_global_device_ids=true | all-gather | bytes 10240 | tf_op jit(solution)/shard_map/all_gather | solution.py:95
  25.9 0.7 reshape.11
  26.6 11.2 %all_gather.14.x_ref = bf16[256,1536]{1,0:T(8,128)(2,1)} all-gather(bf16[64,1536]{1,0:T(8,128)(2,1)} %param.8), channel_id=1, replica_groups=mesh['dp'=2,'ep'=4] {'ep'}, dimensions={0}, use_global_device_ids=true | all-gather | bytes 983040 | tf_op jit(solution)/shard_map/all_gather | solution.py:96
  37.7 11.5 %all_gather.15.dy_ref = bf16[256,1536]{1,0:T(8,128)(2,1)} all-gather(bf16[64,1536]{1,0:T(8,128)(2,1)} %param.9), channel_id=1, replica_groups=mesh['dp'=2,'ep'=4] {'ep'}, dimensions={0}, use_global_device_ids=true | all-gather | bytes 983040 | tf_op jit(solution)/shard_map/all_gather | solution.py:97
  49.2 56.6 %experts.1 = (f32[256,1536]{1,0:T(8,128)}, f32[10,1536,512]{2,1,0:T(8,128)}, f32[10,512,1536]{2,1,0:T(8,128)}, f32[10,1536,512]{2,1,0:T(8,128)}) custom-call(s32[8,256]{1,0:T(8,128)} %bitcast.9, f32[8,256]{1,0:T(8,128)} %bitcast.10, bf16[256,1536]{1,0:T(8,128)(2,1)} %all_gather.14.x_ref, bf16[256,1536]{1,0:T(8,128)(2,1)} %all_gather.15.dy_ref, ...), custom_call_target="tpu_custom_call" | custom-call | flops 12079595520 | bytes 141557760 | tf_op jit(solution)/shard_map/experts/pallas_call | solution.py:100
  105.9 0.0 reduce-scatter.2.cloned.1.call-update
  105.9 24.0 %reduce-scatter.2.cloned.1.call-done = f32[64,1536]{1,0:T(8,128)} async-done(((f32[256,1536]{1,0:T(8,128)}), f32[64,1536]{1,0:T(8,128)}) %reduce-scatter.2.cloned.1.call-update) | async-done | bytes 393232 | tf_op jit(solution)/shard_map/reduce_scatter | solution.py:122
  129.9 1.7 %convert_element_type.3 = bf16[64,1536]{1,0:T(8,128)(2,1)} convert(f32[64,1536]{1,0:T(8,128)} %reduce-scatter.2.cloned.1.call-done) | non-fusion elementwise | flops 98304 | bytes 589824 | tf_op jit(solution)/shard_map/convert_element_type | solution.py:122
  (2 shorter events, 0.0 us)
Async XLA Ops:
  7.2 122.7 %reduce-scatter.2.cloned.1.call-start = ((), (), s32[]{:S(2)}) async-start(), calls=%async_computation.1 | async-start | bytes 1966080 | tf_op jit(solution)/shard_map/reduce_scatter | solution.py:122
Sparse Core Ops, SparseCore 0:
  106.0 23.7 reduce-scatter.1

commit v2 on v1

v2 whole, which is shorter than its diff:
```python
import functools

import jax
import jax.numpy as jnp
import numpy as np
from jax import lax
from jax.experimental import pallas as pl
from jax.experimental.pallas import tpu as pltpu
from jax.sharding import PartitionSpec as P

F32, BF16 = jnp.float32, jnp.bfloat16
MESH = pl.DeviceIdType.MESH
TN = (((0,), (0,)), ((), ()))
NT = (((1,), (1,)), ((), ()))
DONE_FIRST = 5
SECOND = 1
MIB = 1024 * 1024


def slot_capacity(tok_dev, top_k, n_exp):
    return ((3 * tok_dev * top_k) // (2 * n_exp) + 7) // 8 * 8


def dot(a, b, dims=None):
    if dims is None:
        return jnp.dot(a, b, preferred_element_type=F32)
    return lax.dot_general(a, b, dims, preferred_element_type=F32)


def gather_kernel(meta_ref, x_ref, dy_ref, meta_out, x_out, dy_out, send_sem, recv_sem):
    dp, me = lax.axis_index('dp'), lax.axis_index('ep')
    partner = me + 1 - 2 * lax.rem(me, 2)
    twin = lax.rem(me + 2, 4)
    barrier = pltpu.get_barrier_semaphore()
    for peer in (partner, twin):
        pl.semaphore_signal(barrier, inc=1, device_id=(dp, peer), device_id_type=MESH)
    pl.semaphore_wait(barrier, 2)

    def copy(src, dst, slot, peer, k):
        return pltpu.make_async_remote_copy(src_ref=src, dst_ref=dst.at[slot], send_sem=send_sem.at[k], recv_sem=recv_sem.at[k],
                                            device_id=(dp, peer), device_id_type=MESH)

    pairs = ((meta_ref, meta_out), (x_ref, x_out), (dy_ref, dy_out))
    cross = [copy(src, dst, me, twin, 3 * n) for n, (src, dst) in enumerate(pairs)]
    near = [copy(src, dst, me, partner, 3 * n + 1) for n, (src, dst) in enumerate(pairs)]
    for c in cross:
        c.start()
    for c in near:
        c.start()
    for src, dst in pairs:
        dst[me] = src[...]
    onward = []
    for n, (src, dst) in enumerate(pairs):
        cross[n].wait_recv()
        c = copy(dst.at[twin], dst, twin, partner, 3 * n + 2)
        c.start()
        onward.append(c)
    for c in near + onward:
        c.wait_recv()
    for c in cross + near + onward:
        c.wait_send()


def gather_tokens(meta, x_loc, dy_loc, n_dev):
    vmem = pl.BlockSpec(memory_space=pltpu.VMEM)
    args = (meta, x_loc, dy_loc)
    return pl.pallas_call(
        gather_kernel,
        out_shape=[jax.ShapeDtypeStruct((n_dev,) + a.shape, a.dtype) for a in args],
        in_specs=[vmem] * 3,
        out_specs=[vmem] * 3,
        scratch_shapes=[pltpu.SemaphoreType.DMA((9,)), pltpu.SemaphoreType.DMA((9,))],
        compiler_params=pltpu.CompilerParams(collective_id=0, has_side_effects=True, vmem_limit_bytes=8 * MIB),
        name='gather_tokens',
    )(*args)


def build_rows(cfg, meta_ref, x_ref, dy_ref, hot, x_all, dz_all):
    cap, tok_dev, n_dev, n_local, top_k = cfg
    rows, n_tok = n_dev * cap, n_dev * tok_dev
    me = lax.axis_index('ep')
    first = me * n_local
    keys = jnp.concatenate([meta_ref[s, :top_k, :] for s in range(n_dev)], axis=1)
    gates = jnp.concatenate([meta_ref[s, top_k:, :] for s in range(n_dev)], axis=1)
    keys = keys.astype(jnp.int32)
    source = lax.broadcasted_iota(jnp.int32, (1, n_tok), 1) // tok_dev * cap
    row_ids = lax.broadcasted_iota(jnp.int32, (rows, n_tok), 0)
    x = x_ref[...].reshape(n_tok, -1)
    dy = dy_ref[...].reshape(n_tok, -1)
    for e in range(n_local):
        d = keys - (first + e) * cap
        hit = (d >= 0) & (d < cap)
        slot = jnp.sum(jnp.where(hit, d + 1, 0), axis=0, keepdims=True) - 1
        gmap = jnp.sum(jnp.where(hit, gates, 0.0), axis=0, keepdims=True)
        slot = jnp.where(slot >= 0, slot + source, -1)
        mask = row_ids == slot
        gcol = jnp.sum(jnp.where(mask, gmap, 0.0), axis=1, keepdims=True)
        sel = jnp.where(mask, 1.0, 0.0).astype(BF16)
        hot[pl.ds(e * rows, rows), :] = sel
        x_all[e] = dot(sel, x).astype(BF16)
        dz_all[e] = (gcol * dot(sel, dy)).astype(BF16)


def weight_grads(x_ref, dz, h, da, db, dw1_ref, dw2_ref, dw3_ref):
    for c in range(dw1_ref.shape[1] // 256):
        xt = x_ref[:, pl.ds(c * 256, 256)]
        dw1_ref[0, pl.ds(c * 256, 256), :] = dot(xt, da, TN)
        dw3_ref[0, pl.ds(c * 256, 256), :] = dot(xt, db, TN)
    for c in range(dw2_ref.shape[1] // 256):
        dw2_ref[0, pl.ds(c * 256, 256), :] = dot(h[:, c * 256:(c + 1) * 256], dz, TN)


def first_kernel(cfg, expert_of, grad_of, save_of, flag_of, meta_ref, x_ref, dy_ref, w1_ref, w2_ref, w3_ref,
                 keep_ref, send_ref, xs_ref, dzs_ref, hs_ref, das_ref, dbs_ref, dw1_ref, dw2_ref, dw3_ref, hot, x_all, dz_all, dx_all):
    cap, tok_dev, n_dev, n_local, top_k = cfg
    rows = n_dev * cap
    i = pl.program_id(0)
    e = expert_of[i]

    @pl.when(i == 0)
    def _():
        build_rows(cfg, meta_ref, x_ref, dy_ref, hot, x_all, dz_all)

    x = x_all[e]
    dz = dz_all[e]
    a = dot(x, w1_ref[0]).astype(BF16).astype(F32)
    b = dot(x, w3_ref[0]).astype(BF16).astype(F32)
    sg = jax.nn.sigmoid(a)
    silu = a * sg
    h = (silu * b).astype(BF16)
    dh = dot(dz, w2_ref[0], NT)
    da = (dh * b * sg * (1.0 + a * (1.0 - sg))).astype(BF16)
    db = (dh * silu).astype(BF16)
    dx = (dot(da, w1_ref[0], NT) + dot(db, w3_ref[0], NT)).astype(BF16)
    dx_all[pl.ds(pl.multiple_of(e * rows, 16), rows), :] = dx

    @pl.when(flag_of[i] == 1)
    def _():
        weight_grads(x_all.at[e], dz, h, da, db, dw1_ref, dw2_ref, dw3_ref)

    @pl.when(flag_of[i] == 0)
    def _():
        xs_ref[0] = x
        dzs_ref[0] = dz
        hs_ref[0] = h
        das_ref[0] = da
        dbs_ref[0] = db

    @pl.when(i == n_local - 1)
    def _():
        me = lax.axis_index('ep')
        for s in range(n_dev):
            part = dot(hot[:, s * tok_dev:(s + 1) * tok_dev], dx_all[...], TN)
            q = jnp.bitwise_xor(s, me)
            half = q // 2

            @pl.when(q % 2 == 0)
            def _():
                keep_ref[half] = part

            @pl.when(q % 2 == 1)
            def _():
                send_ref[half] = part


def later_kernel(x_ref, dz_ref, h_ref, da_ref, db_ref, i1, i2, i3, dw1_ref, dw2_ref, dw3_ref):
    weight_grads(x_ref.at[0], dz_ref[0], h_ref[0], da_ref[0], db_ref[0], dw1_ref, dw2_ref, dw3_ref)


def grads_cost(n, rows, d_model, ff):
    return pl.CostEstimate(flops=6 * n * rows * d_model * ff, bytes_accessed=12 * n * d_model * ff, transcendentals=0)


def later_grads(saved, grads, start, first, count):
    rows, d_model = saved[0].shape[1:]
    ff = saved[2].shape[2]
    src = lambda shape: pl.BlockSpec((1,) + shape, lambda i: (start + i, 0, 0))
    dst = lambda shape: pl.BlockSpec((1,) + shape, lambda i: (first + start + i, 0, 0))
    return pl.pallas_call(
        later_kernel,
        grid=(count,),
        out_shape=[jax.ShapeDtypeStruct(g.shape, g.dtype) for g in grads],
        in_specs=[src((rows, d_model)), src((rows, d_model)), src((rows, ff)), src((rows, ff)), src((rows, ff))] + [pl.BlockSpec(memory_space=pl.ANY)] * 3,
        out_specs=[dst((d_model, ff)), dst((ff, d_model)), dst((d_model, ff))],
        input_output_aliases={5: 0, 6: 1, 7: 2},
        compiler_params=pltpu.CompilerParams(dimension_semantics=('arbitrary',), vmem_limit_bytes=32 * MIB),
        cost_estimate=grads_cost(count, rows, d_model, ff),
        name='later_grads',
    )(*saved, *grads)


def schedule(n_local, done):
    flags, acc = [], 0
    for i in range(n_local):
        acc += done
        flags.append(1 if acc >= n_local or i == 0 and done else 0)
        if flags[-1]:
            acc -= n_local
    while sum(flags) > done:
        flags[len(flags) - 1 - flags[::-1].index(1)] = 0
    n_done = n_save = 0
    expert, grad, save = [], [], []
    for f in flags:
        expert.append(n_done if f else done + n_save)
        grad.append(min(n_done, max(done - 1, 0)))
        save.append(min(n_save, max(n_local - done - 1, 0)))
        n_done += f
        n_save += 1 - f
    return [np.asarray(v, np.int32) for v in (expert, grad, save, flags)]


def first_experts(cfg, meta, x_tok, dy_tok, w_gate, w_down, w_up, done):
    cap, tok_dev, n_dev, n_local, top_k = cfg
    d_model, ff = w_gate.shape[1:]
    rows, n_tok, left = n_dev * cap, n_dev * tok_dev, n_local - done
    vmem = pl.BlockSpec(memory_space=pltpu.VMEM)
    per = lambda shape: pl.BlockSpec((1,) + shape, lambda i, ex, gr, sa, fl: (ex[i], 0, 0))
    grad = lambda shape: pl.BlockSpec((1,) + shape, lambda i, ex, gr, sa, fl: (gr[i], 0, 0))
    save = lambda shape: pl.BlockSpec((1,) + shape, lambda i, ex, gr, sa, fl: (sa[i], 0, 0))
    out = jax.ShapeDtypeStruct
    return pl.pallas_call(
        functools.partial(first_kernel, cfg),
        grid_spec=pltpu.PrefetchScalarGridSpec(
            num_scalar_prefetch=4,
            grid=(n_local,),
            in_specs=[vmem, vmem, vmem, per((d_model, ff)), per((ff, d_model)), per((d_model, ff))],
            out_specs=[vmem, vmem, save((rows, d_model)), save((rows, d_model)), save((rows, ff)), save((rows, ff)), save((rows, ff)),
                       grad((d_model, ff)), grad((ff, d_model)), grad((d_model, ff))],
            scratch_shapes=[
                pltpu.VMEM((n_local * rows, n_tok), BF16),
                pltpu.VMEM((n_local, rows, d_model), BF16),
                pltpu.VMEM((n_local, rows, d_model), BF16),
                pltpu.VMEM((n_local * rows, d_model), BF16),
            ],
        ),
        out_shape=[
            out((2, tok_dev, d_model), F32), out((2, tok_dev, d_model), F32),
            out((left, rows, d_model), BF16), out((left, rows, d_model), BF16), out((left, rows, ff), BF16), out((left, rows, ff), BF16), out((left, rows, ff), BF16),
            out((n_local, d_model, ff), F32), out((n_local, ff, d_model), F32), out((n_local, d_model, ff), F32),
        ],
        compiler_params=pltpu.CompilerParams(dimension_semantics=('arbitrary',), vmem_limit_bytes=46 * MIB),
        cost_estimate=pl.CostEstimate(flops=16 * n_local * rows * d_model * ff, bytes_accessed=12 * n_local * d_model * ff, transcendentals=0),
        name='first_experts',
    )(*schedule(n_local, done), meta, x_tok, dy_tok, w_gate, w_down, w_up)


def solution(mesh):
    n_dev = mesh.shape['ep']

    def local_step(x_loc, dy_loc, ids_loc, gate_loc, slot_loc, w_gate, w_down, w_up):
        tok_dev, top_k = ids_loc.shape
        n_local, d_model, ff = w_gate.shape
        cap = slot_capacity(tok_dev, top_k, n_local * n_dev)
        cfg = (cap, tok_dev, n_dev, n_local, top_k)
        keys = jnp.where(slot_loc >= 0, ids_loc * cap + slot_loc, -1).astype(F32)
        meta = jnp.concatenate([keys.T, gate_loc.T], axis=0)
        meta, x_tok, dy_tok = gather_tokens(meta, x_loc, dy_loc, n_dev)
        done = DONE_FIRST
        keep, send, *rest = first_experts(cfg, meta, x_tok, dy_tok, w_gate, w_down, w_up, done)
        saved, grads = rest[:5], rest[5:]
        got = lax.ppermute(send, 'ep', [(d, d ^ 1) for d in range(n_dev)])
        grads = later_grads(saved, grads, 0, done, SECOND)
        cross = lax.ppermute(keep[1] + got[1], 'ep', [(d, d ^ 2) for d in range(n_dev)])
        grads = later_grads(saved, grads, SECOND, done, n_local - done - SECOND)
        dx = (keep[0] + got[0] + cross).astype(BF16)
        return dx, *grads

    tok_spec = P(('dp', 'ep'), None)
    w_spec = P('ep', None, None)
    grad_spec = P(('dp', 'ep'), None, None)
    return jax.shard_map(local_step, mesh=mesh, in_specs=(tok_spec, tok_spec, tok_spec, tok_spec, tok_spec, w_spec, w_spec, w_spec), out_specs=(tok_spec, grad_spec, grad_spec, grad_spec), check_vma=False)
```

time: 139 us -> 98.7 us (0.71)
  blocking collectives: 39.9 us -> 0 us
  Pallas kernels: 56.6 us -> 87.7 us
  waiting for transfers between devices: 24 us -> 1.91 us
  between operations: 14 us -> 0.66 us
  local copies, waits for them, and re-layouts: 1.37 us -> 4.47 us
  starting transfers between devices: 0.04 us -> 1.48 us
    all_gather x4 -> x0, blocking collectives: 39.9 us -> none  [the longest x1 11.5 us: local_step(): dy_tok = lax.all_gather(dy_loc, 'ep', axis=0, tiled=True)]
    pallas_call x1 -> x4, Pallas kernels: 56.6 us -> 87.7 us  [the longest x1 55.1 us: first_experts(): pl.pallas_call(functools.partial(first_kernel, cfg), grid_spec=pltpu.Pref...]
    reduce_scatter x1 -> x0, waiting for transfers between devices: 24 us -> none  [local_step(): lax.psum_scatter(part, 'ep', scatter_dimension=0, tiled=True).astype(BF16)]
    unnamed x2 -> x12, local copies, waits for them, and re-layouts: 1.36 us -> 4.47 us
    ppermute x0 -> x2, waiting for transfers between devices: none -> 1.91 us  [the longest x1 1.91 us: local_step(): got = lax.ppermute(send, 'ep', [(d, d ^ 1) for d in range(n_dev)])]
    ppermute x0 -> x2, starting transfers between devices: none -> 1.48 us  [the longest x1 1.09 us: local_step(): lax.ppermute(keep[1] + got[1], 'ep', [(d, d ^ 2) for d in range(n_dev)])]
  transfers between devices with their start and end apart: 1 -> 2, of which waited for: 1 -> 1; matrix products, arithmetic and copies ran while one was open for 0% -> 0% of each run, Pallas kernels for 0% -> 18%
where the time goes in v2:
time: 98.7 us; the launch traced here: 98.4 us
  Pallas kernels  87.7 us (89%)
  local copies, waits for them, and re-layouts  4.47 us (5%)
  other arithmetic  2.18 us (2%)
  waiting for transfers between devices  1.91 us (2%)
  starting transfers between devices  1.48 us (1%)
    pallas_call x1, Pallas kernels, first_experts(): pl.pallas_call(functools.partial(first_kernel, cfg), grid_spec=pltpu.Pref...  55.1 us
    pallas_call x2, Pallas kernels, later_grads(): pl.pallas_call(later_kernel, grid=(count,), out_shape=[jax.ShapeDtypeStru...  18.1 us
    pallas_call x1, Pallas kernels, gather_tokens(): pl.pallas_call(gather_kernel, out_shape=[jax.ShapeDtypeStruct((n_dev,) +...  14.5 us
    unnamed x12, local copies, waits for them, and re-layouts  4.47 us
  transfers between devices with their start and end apart: 2, of which 1 were waited for; matrix products, arithmetic and copies ran while one was open for 0% of the time, Pallas kernels for 18%

profile of v2, /device:TPU:0, one launch (start us, length us, event | category | flops | bytes accessed | tf_op | source)
XLA Modules:
  0.0 98.4 jit_solution(12921146858518545440)
XLA Ops:
  0.6 0.7 convert_bitcast_fusion
  1.3 0.7 pad_maximum_fusion.meta_ref
  2.0 0.0 copy-start
  2.0 0.9 copy-done
  3.0 0.0 copy-start.1
  3.0 0.9 copy-done.1
  3.9 14.5 %gather_tokens.1 = (f32[4,16,64]{2,1,0:T(8,128)S(1)}, bf16[4,64,1536]{2,1,0:T(8,128)(2,1)S(1)}, bf16[4,64,1536]{2,1,0:T(8,128)(2,1)S(1)}) custom-call(f32[16,64]{1,0:T(8,128)S(1)} %pad_maximum_fusion.meta_ref, bf16[64,1536]{1,0:T(8,128)(2,1)S(1)} %copy-done, bf16[64,1536]{1,0:T(8,128)(2,1)S(1)} %copy-done.1), custom_call_target="tpu_custom_call" | custom-call | tf_op jit(solution)/shard_map/gather_tokens/pallas_call | solution.py:67
  18.4 0.0 copy-start.2
  18.4 0.6 copy-done.2
  19.1 0.0 copy-start.3
  19.1 0.7 copy-done.3
  19.7 0.0 copy-start.4
  19.7 0.7 copy-done.4
  20.4 0.0 copy-start.5
  20.4 0.7 copy-done.5
  21.1 55.1 %first_experts.1 = (f32[2,64,1536]{2,1,0:T(8,128)S(1)}, f32[2,64,1536]{2,1,0:T(8,128)S(1)}, bf16[5,96,1536]{2,1,0:T(8,128)(2,1)S(1)}, bf16[5,96,1536]{2,1,0:T(8,...) custom-call(s32[10]{0:T(128)S(1)} %copy-done.5, ...), custom_call_target="tpu_custom_call" | custom-call | flops 12079595520 | bytes 94371840 | tf_op jit(solution)/shard_map/first_experts/pallas_call | solution.py:221
  76.2 0.4 collective-permute-start
  76.6 1.9 %collective-permute-done = f32[2,64,1536]{2,1,0:T(8,128)S(1)} collective-permute-done((f32[2,64,1536]{2,1,0:T(8,128)S(1)}, f32[2,64,1536]{2,1,0:T(8,128)S(1)}, u32[]{:S(2)}, u32[]{:S(2)}) %collective-permute-start) | collective-permute-done | bytes 786464 | tf_op jit(solution)/shard_map/ppermute | solution.py:261
  78.5 1.1 %collective-permute-start.1 = (f32[64,1536]{1,0:T(8,128)S(1)}, f32[64,1536]{1,0:T(8,128)S(1)}, u32[]{:S(2)}, u32[]{:S(2)}) collective-permute-start(f32[64,1536]{1,0:T(8,128)S(1)} %fusion), channel_id=1, source_target_pairs={{0,2},{1,3},{2,0},{3,1},{4,6},{5,7},{6,4},{7,5}} | collective-permute-start | bytes 1179656 | tf_op jit(solution)/shard_map/ppermute | solution.py:263
  79.6 4.7 %later_grads.2 = (f32[10,1536,512]{2,1,0:T(8,128)}, f32[10,512,1536]{2,1,0:T(8,128)}, f32[10,1536,512]{2,1,0:T(8,128)}) custom-call(bf16[5,96,1536]{2,1,0:T(8,128)(2,1)S(1)} %get-tuple-element.28.x_ref, bf16[5,96,1536]{2,1,0:T(8,128)(2,1)S(1)} %get-tuple-element.29.dz_ref, ...), custom_call_target="tpu_custom_call", output_to_operand_aliasing={{0}: (5, {}), {1}: (6, {}), {2}: (7, {})} | custom-call | flops 452984832 | bytes 9437184 | tf_op jit(solution)/shard_map/later_grads/pallas_call | solution.py:179
  84.3 13.4 %later_grads.3 = (f32[10,1536,512]{2,1,0:T(8,128)}, f32[10,512,1536]{2,1,0:T(8,128)}, f32[10,1536,512]{2,1,0:T(8,128)}) custom-call(bf16[5,96,1536]{2,1,0:T(8,128)(2,1)S(1)} %get-tuple-element.28.x_ref, bf16[5,96,1536]{2,1,0:T(8,128)(2,1)S(1)} %get-tuple-element.29.dz_ref, ...), custom_call_target="tpu_custom_call", output_to_operand_aliasing={{0}: (5, {}), {1}: (6, {}), {2}: (7, {})} | custom-call | flops 1811939328 | bytes 37748736 | tf_op jit(solution)/shard_map/later_grads/pallas_call | solution.py:179
  97.7 0.0 collective-permute-done.1
  97.7 0.7 fusion.3
  (1 shorter events, 0.0 us)
Async XLA Ops:
  2.0 0.9 copy-start
  3.0 0.9 copy-start.1
  18.4 0.7 copy-start.2
  19.1 0.7 copy-start.3
  19.7 0.7 copy-start.4
  20.4 0.7 copy-start.5
  76.2 2.3 %collective-permute-start = (f32[2,64,1536]{2,1,0:T(8,128)S(1)}, f32[2,64,1536]{2,1,0:T(8,128)S(1)}, u32[]{:S(2)}, u32[]{:S(2)}) collective-permute-start(f32[2,64,1536]{2,1,0:T(8,128)S(1)} %get-tuple-element.27), channel_id=1, source_target_pairs={{0,1},{1,0},{2,3},{3,2},{4,5},{5,4},{6,7},{7,6}} | collective-permute-start | bytes 2359304 | tf_op jit(solution)/shard_map/ppermute | solution.py:261
  78.5 19.2 %collective-permute-start.1 = (f32[64,1536]{1,0:T(8,128)S(1)}, f32[64,1536]{1,0:T(8,128)S(1)}, u32[]{:S(2)}, u32[]{:S(2)}) collective-permute-start(f32[64,1536]{1,0:T(8,128)S(1)} %fusion), channel_id=1, source_target_pairs={{0,2},{1,3},{2,0},{3,1},{4,6},{5,7},{6,4},{7,5}} | collective-permute-start | bytes 1179656 | tf_op jit(solution)/shard_map/ppermute | solution.py:263
